TPU v7x, 32 devices: a whole 2x2x4 slice. The times are simulated.
32 devices in a mesh: wide: 8 (over y, x, core), head: 4 (over z).
Axes of the slice: x: 2, y: 2, z: 4, core: 2. Of those that a mesh axis runs over, the one named last changes fastest.
Arguments:
- tokens: bfloat16 [16384, 1024], P(('wide', 'head')), may hold values from -6 to 6
- cotangent: bfloat16 [16384, 1024], P(('wide', 'head')), may hold values from -6 to 6
- w_query: bfloat16 [1024, 1024], P('wide', 'head'), may hold values from -0.25 to 0.25
- w_key: bfloat16 [1024, 1024], P('wide', 'head'), may hold values from -0.25 to 0.25
- w_value: bfloat16 [1024, 1024], P('wide', 'head'), may hold values from -0.1875 to 0.1875
- w_out: bfloat16 [1024, 1024], P('head', 'wide'), may hold values from -0.1875 to 0.1875
- w_up: bfloat16 [1024, 4096], P('wide', 'head'), may hold values from -0.1875 to 0.1875
- w_down: bfloat16 [4096, 1024], P('head', 'wide'), may hold values from -0.09375 to 0.09375
- norm_gain: float32 [4, 1024], replicated, may hold values from 0.25 to 1.75
- norm_bias: float32 [4, 1024], replicated, may hold values from -3 to 3
Outputs:
- block_out: bfloat16 [16384, 1024], P(('wide', 'head'))
- input_grad: float32 [16384, 1024], P(('wide', 'head'))
- grad_query: float32 [1024, 1024], P('wide', 'head')
- grad_key: float32 [1024, 1024], P('wide', 'head')
- grad_value: float32 [1024, 1024], P('wide', 'head')
- grad_out: float32 [1024, 1024], P('head', 'wide')
- grad_up: float32 [1024, 4096], P('wide', 'head')
- grad_down: float32 [4096, 1024], P('head', 'wide')
- gain_grad: float32 [4, 1024], replicated
- bias_grad: float32 [4, 1024], replicated
All inputs are finite; a program needn't handle non-finite values.
Results may differ from a plain program's by a relative error of at most 0.015.
Values may be sent and summed in bfloat16 or wider, within the bound.
No kernel may reach another device: no remote copies, remote signals or barrier semaphores. Data moves between devices by JAX's collectives and lax.ppermute only.
A program may use at most 192 MiB of HBM per device.

v0:
```python
import math
import jax
import jax.numpy as jnp
from jax import lax
from jax.sharding import Mesh, PartitionSpec as P

HD = 64
EPS = 1e-05


def normalize(values, gain, bias):
    average = jnp.mean(values, axis=-1, keepdims=True)
    centred = values - average
    inverse = lax.rsqrt(jnp.mean(centred * centred, axis=-1, keepdims=True) + EPS)
    unit_rows = centred * inverse
    return (unit_rows * gain + bias, unit_rows, inverse)


def normalize_back(gradient, unit_rows, inverse, gain):
    scaled = gradient * gain
    inner_sum = (
        scaled
        - jnp.mean(scaled, axis=-1, keepdims=True)
        - unit_rows * jnp.mean(scaled * unit_rows, axis=-1, keepdims=True)
    )
    return (inner_sum * inverse, jnp.sum(gradient * unit_rows, axis=0), jnp.sum(gradient, axis=0))


def masked_scores(rows_q, key_heads, first_row, score_scale):
    scores = (
        jnp.einsum("qgd,kgd->gqk", rows_q, key_heads, preferred_element_type=jnp.float32)
        * score_scale
    )
    place_q = first_row + jnp.arange(rows_q.shape[0], dtype=jnp.int32)
    place_k = jnp.arange(key_heads.shape[0], dtype=jnp.int32)
    allowed = place_k[None, :] <= place_q[:, None]
    return jnp.where(allowed[None], scores, -1e30)


def attend(queries, key_rows, value_rows, block_rows):
    length, width = queries.shape
    groups = width // HD
    score_scale = 1.0 / math.sqrt(HD)
    query_heads = queries.reshape(length, groups, HD)
    key_heads = key_rows.reshape(length, groups, HD)
    value_heads = value_rows.reshape(length, groups, HD)
    out_blocks = []
    totals = []
    for position in range(length // block_rows):
        first_row = position * block_rows
        last_row = first_row + block_rows
        scores = masked_scores(
            query_heads[first_row:last_row], key_heads[:last_row], first_row, score_scale
        )
        row_max = jnp.max(scores, axis=-1, keepdims=True)
        exp_scores = jnp.exp(scores - row_max)
        row_total = jnp.sum(exp_scores, axis=-1, keepdims=True)
        weights = (exp_scores / row_total).astype(jnp.bfloat16)
        out_blocks.append(
            jnp.einsum(
                "gqk,kgd->qgd", weights, value_heads[:last_row], preferred_element_type=jnp.float32
            )
        )
        totals.append(row_max + jnp.log(row_total))
    return (jnp.concatenate(out_blocks, axis=0).reshape(length, width), totals)


def attend_back(queries, key_rows, value_rows, grad_rows, totals, block_rows):
    length, width = queries.shape
    groups = width // HD
    score_scale = 1.0 / math.sqrt(HD)
    query_heads = queries.reshape(length, groups, HD)
    key_heads = key_rows.reshape(length, groups, HD)
    value_heads = value_rows.reshape(length, groups, HD)
    grad_heads = grad_rows.reshape(length, groups, HD)
    grad_keys = jnp.zeros((length, groups, HD), jnp.float32)
    grad_values = jnp.zeros((length, groups, HD), jnp.float32)
    query_parts = []
    for position in range(length // block_rows):
        first_row = position * block_rows
        last_row = first_row + block_rows
        rows_q = query_heads[first_row:last_row]
        scores = masked_scores(rows_q, key_heads[:last_row], first_row, score_scale)
        weights = jnp.exp(scores - totals[position])
        rounded = weights.astype(jnp.bfloat16)
        grad_block = grad_heads[first_row:last_row]
        grad_values = grad_values.at[:last_row].add(
            jnp.einsum("gqk,qgd->kgd", rounded, grad_block, preferred_element_type=jnp.float32)
        )
        grad_weights = jnp.einsum(
            "qgd,kgd->gqk", grad_block, value_heads[:last_row], preferred_element_type=jnp.float32
        )
        inner_sum = jnp.sum(weights * grad_weights, axis=-1, keepdims=True)
        grad_scores = (weights * (grad_weights - inner_sum)).astype(jnp.bfloat16)
        query_parts.append(
            jnp.einsum(
                "gqk,kgd->qgd",
                grad_scores,
                key_heads[:last_row],
                preferred_element_type=jnp.float32,
            )
            * score_scale
        )
        grad_keys = grad_keys.at[:last_row].add(
            jnp.einsum("gqk,qgd->kgd", grad_scores, rows_q, preferred_element_type=jnp.float32)
            * score_scale
        )
    grad_queries = jnp.concatenate(query_parts, axis=0).reshape(length, width).astype(jnp.bfloat16)
    return (
        grad_queries,
        grad_keys.reshape(length, width).astype(jnp.bfloat16),
        grad_values.reshape(length, width).astype(jnp.bfloat16),
    )


def contract_rows(left_op, right_op):
    return lax.dot_general(
        left_op, right_op, (((0,), (0,)), ((), ())), preferred_element_type=jnp.float32
    )


def contract_cols(left_op, right_op):
    return lax.dot_general(
        left_op, right_op, (((1,), (1,)), ((), ())), preferred_element_type=jnp.float32
    )


WIDE = ("outer", "pair")
ALL = ("outer", "pair", "head")


def swap(values):
    return lax.ppermute(values, "pair", [(0, 1), (1, 0)])


def halves(block, axis):
    size = block.shape[axis] // 2
    place = lax.axis_index("pair")
    own = lax.dynamic_slice_in_dim(block, place * size, size, axis)
    other = lax.dynamic_slice_in_dim(block, (1 - place) * size, size, axis)
    return (own, other)


def in_order(own, other, axis):
    place = lax.axis_index("pair")
    return jnp.where(
        place == 0,
        jnp.concatenate([own, other], axis=axis),
        jnp.concatenate([other, own], axis=axis),
    )


def gather_half(block):
    own, other = halves(block, 1)
    pair_rows = in_order(own, swap(other), 0)
    columns = lax.all_gather(pair_rows, "head", axis=0, tiled=False)
    columns = columns.transpose(1, 0, 2).reshape(pair_rows.shape[0], -1)
    return lax.all_gather(columns, "outer", axis=0, tiled=True)


def scatter_half(grad, groups):
    rows = lax.psum_scatter(grad, "outer", scatter_dimension=0, tiled=True)
    blocks = rows.reshape(rows.shape[0], groups, -1).transpose(1, 0, 2)
    block = lax.psum_scatter(blocks, "head", scatter_dimension=0, tiled=False)
    own, other = halves(block, 0)
    return in_order(own, swap(other), 1)


def on_device(
    tokens, cotangent, w_query, w_key, w_value, w_out, w_up, w_down, norm_gain, norm_bias
):
    groups = lax.axis_size("head")
    rows = tokens.shape[0]
    width = w_query.shape[1]
    bf16 = jnp.bfloat16
    w_attn = lax.all_gather(
        jnp.concatenate([w_query, w_key, w_value], axis=1), WIDE, axis=0, tiled=True
    )
    residual = tokens.astype(jnp.float32)
    norm_a, unit_a, inv_a = normalize(residual, norm_gain[0], norm_bias[0])
    seq_a = lax.all_gather(norm_a.astype(bf16), "head", axis=0, tiled=True)
    full_o = lax.all_gather(
        lax.all_gather(w_out, "head", axis=0, tiled=True).T, WIDE, axis=0, tiled=True
    )
    full_up = gather_half(w_up)
    full_down = gather_half(w_down.T)
    block_rows = min(512, seq_a.shape[0])
    qkv = jnp.dot(seq_a, w_attn, preferred_element_type=jnp.float32).astype(bf16)
    queries, key_rows, value_rows = (qkv[:, i * width : (i + 1) * width] for i in range(3))
    attended, totals = attend(queries, key_rows, value_rows, block_rows)
    attended = lax.all_to_all(
        attended.astype(bf16).reshape(groups, rows, width), "head", 0, 0, tiled=False
    )
    attended = attended.transpose(1, 0, 2).reshape(rows, groups * width)
    mixed = contract_cols(attended, full_o)
    norm_z, unit_z, inv_z = normalize(mixed, norm_gain[1], norm_bias[1])
    hidden = residual + norm_z
    norm_c, unit_c, inv_c = normalize(hidden, norm_gain[2], norm_bias[2])
    rows_c = norm_c.astype(bf16)
    pair_c = jnp.concatenate([rows_c, swap(rows_c)], axis=0)
    pre_act = jnp.dot(pair_c, full_up, preferred_element_type=jnp.float32)
    active, gelu_back = jax.vjp(jax.nn.gelu, pre_act)
    active = active.astype(bf16)
    both = contract_cols(active, full_down)
    output = both[:rows] + swap(both[rows:].astype(bf16)).astype(jnp.float32)
    norm_m, unit_m, inv_m = normalize(output, norm_gain[3], norm_bias[3])
    block_out = (hidden + norm_m).astype(bf16)
    grad_y = cotangent.astype(jnp.float32)
    grad_m, gain_m, bias_m = normalize_back(grad_y, unit_m, inv_m, norm_gain[3])
    rows_gm = grad_m.astype(bf16)
    pair_gm = jnp.concatenate([rows_gm, swap(rows_gm)], axis=0)
    grad_act = jnp.dot(pair_gm, full_down, preferred_element_type=jnp.float32)
    grad_pre = gelu_back(grad_act)[0].astype(bf16)
    both_c = contract_cols(grad_pre, full_up)
    grad_c = both_c[:rows] + swap(both_c[rows:].astype(bf16)).astype(jnp.float32)
    grad_down = scatter_half(contract_rows(pair_gm, active).astype(bf16), groups).T
    grad_up = scatter_half(contract_rows(pair_c, grad_pre).astype(bf16), groups)
    grad_more, gain_c, bias_c = normalize_back(grad_c, unit_c, inv_c, norm_gain[2])
    grad_h = grad_y + grad_more
    grad_z, gain_z, bias_z = normalize_back(grad_h, unit_z, inv_z, norm_gain[1])
    rows_gz = grad_z.astype(bf16)
    grad_att = jnp.dot(rows_gz, full_o, preferred_element_type=jnp.float32).astype(bf16)
    grad_att = grad_att.reshape(rows, groups, width).transpose(1, 0, 2)
    grad_att = lax.all_to_all(grad_att, "head", 0, 0, tiled=False)
    grad_att = grad_att.reshape(groups * rows, width)
    grad_o = contract_rows(rows_gz, attended).astype(bf16)
    grad_o = lax.psum_scatter(grad_o, WIDE, scatter_dimension=0, tiled=True)
    grad_o = grad_o.T.reshape(groups, width, -1)
    grad_o = lax.psum_scatter(grad_o, "head", scatter_dimension=0, tiled=False)
    grad_queries, grad_keys, grad_values = attend_back(
        queries, key_rows, value_rows, grad_att, totals, block_rows
    )
    grad_qkv = jnp.concatenate([grad_queries, grad_keys, grad_values], axis=1)
    grad_a = contract_cols(grad_qkv, w_attn).astype(bf16)
    grad_a = lax.psum_scatter(grad_a, "head", scatter_dimension=0, tiled=True).astype(jnp.float32)
    grad_w = contract_rows(seq_a, grad_qkv).astype(bf16)
    grad_w = lax.psum_scatter(grad_w, WIDE, scatter_dimension=0, tiled=True).astype(jnp.float32)
    grad_first, gain_a, bias_a = normalize_back(grad_a, unit_a, inv_a, norm_gain[0])
    input_grad = grad_h + grad_first
    gain_grad, bias_grad = lax.psum(
        (jnp.stack([gain_a, gain_z, gain_c, gain_m]), jnp.stack([bias_a, bias_z, bias_c, bias_m])),
        ALL,
    )
    return (
        block_out,
        input_grad,
        grad_w[:, :width],
        grad_w[:, width : 2 * width],
        grad_w[:, 2 * width :],
        grad_o.astype(jnp.float32),
        grad_up.astype(jnp.float32),
        grad_down.astype(jnp.float32),
        gain_grad,
        bias_grad,
    )


def solution(mesh):
    wide, head = (mesh.shape["wide"], mesh.shape["head"])
    paired = Mesh(mesh.devices.reshape(wide // 2, 2, head), ALL)
    rows = P(ALL, None)
    by_rows = P(WIDE, "head")
    by_cols = P("head", WIDE)
    in_specs = (rows, rows, by_rows, by_rows, by_rows, by_cols, by_rows, by_cols, P(), P())
    out_specs = (rows, rows, by_rows, by_rows, by_rows, by_cols, by_rows, by_cols, P(), P())
    return jax.shard_map(
        on_device, mesh=paired, in_specs=in_specs, out_specs=out_specs, check_vma=False
    )
```

profile of v0, /device:TPU:0, one launch (start us, length us, event | category | flops | bytes accessed | tf_op | source)
XLA Modules:
  0.0 775.5 jit_solution(3823945687830756972)
XLA Ops:
  18.0 18.6 %all_gather.28 = bf16[1024,128]{1,0:T(8,128)(2,1)} all-gather(bf16[256,128]{1,0:T(8,128)(2,1)S(1)} %copy-done.59), channel_id=1, replica_groups=mesh['outer'=4,'pair'=2,'head'=4] {'head'}, dimensions={0}, use_global_device_ids=true | all-gather | bytes 327680 | tf_op jit(solution)/shard_map/all_gather | solution.py:183
  36.7 9.3 %all-gather.14.cloned.1.call-done = bf16[4,256,512]{2,1,0:T(8,128)(2,1)} async-done(((bf16[1,256,512]{2,1,0:T(8,128)(2,1)}), bf16[4,256,512]{2,1,0:T(8,128)(2,1)}) %all-gather.14.cloned.1.call-update) | async-done | bytes 1048592 | tf_op jit(solution)/shard_map/all_gather | solution.py:156
  52.6 22.5 %all-gather.18.cloned.1.call-done = bf16[4,256,512]{2,1,0:T(8,128)(2,1)} async-done(((bf16[1,256,512]{2,1,0:T(8,128)(2,1)}), bf16[4,256,512]{2,1,0:T(8,128)(2,1)}) %all-gather.18.cloned.1.call-update) | async-done | bytes 1048592 | tf_op jit(solution)/shard_map/all_gather | solution.py:156
  77.4 24.6 %all-gather.10.cloned.1.call-done = bf16[1024,768]{1,0:T(8,128)(2,1)} async-done(((bf16[128,768]{1,0:T(8,128)(2,1)}), bf16[1024,768]{1,0:T(8,128)(2,1)}) %all-gather.10.cloned.1.call-update) | async-done | bytes 1572880 | tf_op jit(solution)/shard_map/all_gather | solution.py:176
  102.0 82.8 %all-gather.8.cloned.1.call-done = bf16[2048,1024]{1,0:T(8,128)(2,1)} async-done(((bf16[512,1024]{1,0:T(8,128)(2,1)}), bf16[2048,1024]{1,0:T(8,128)(2,1)}) %all-gather.8.cloned.1.call-update) | async-done | bytes 4194320 | tf_op jit(solution)/shard_map/all_gather | solution.py:181
  223.6 8.4 %fusion = f32[4,512]{1,0:T(4,128)S(1)} fusion(f32[4,512,2048]{2,1,0:T(8,128)} %get-tuple-element.223, f32[4,512]{1,0:T(4,128)S(1)} %get-tuple-element.222), kind=kLoop, calls=%fused_computation.6 | loop fusion | flops 8386560 | bytes 16793600 | tf_op jit(solution)/shard_map/reduce_sum | solution.py:57
  246.9 25.8 %all-to-all-done = bf16[4,512,256]{1,2,0:T(8,128)(2,1)S(1)} async-done(((bf16[4,512,256]{1,2,0:T(8,128)(2,1)}), bf16[4,512,256]{1,2,0:T(8,128)(2,1)S(1)}, u32[]{:S(2)}, u32[]{:S(2)}) %all-to-all-start) | async-done | bytes 1048608 | tf_op jit(solution)/shard_map/all_to_all | solution.py:191
  280.7 10.3 %fusion.85 = f32[1024,2048]{1,0:T(8,128)} fusion(bf16[1024,2048]{0,1:T(8,128)(2,1)} %all-gather.16.cloned.1.call-done, bf16[512,1024]{1,0:T(8,128)(2,1)} %collective-permute-done, bf16[512,1024]{1,0:T(8,128)(2,1)S(1)} %add_convert_fusion.1), kind=kOutput, calls=%fused_computation.139 | convolution fusion | flops 4299161600 | bytes 14680064 | tf_op jit(solution)/shard_map/dot_general | solution.py:201
  291.1 31.1 %all-gather.20.cloned.1.call-done = bf16[1024,2048]{0,1:T(8,128)(2,1)} async-done(((bf16[256,2048]{0,1:T(8,128)(2,1)}), bf16[1024,2048]{0,1:T(8,128)(2,1)}) %all-gather.20.cloned.1.call-update) | async-done | bytes 4194320 | tf_op jit(solution)/shard_map/all_gather | solution.py:158
  322.1 9.0 %fusion.120 = f32[1024,1024]{1,0:T(8,128)S(1)} fusion(bf16[1024,2048]{0,1:T(8,128)(2,1)} %all-gather.20.cloned.1.call-done, f32[1024,2048]{1,0:T(8,128)} %fusion.85), kind=kOutput, calls=%fused_computation.219 | convolution fusion | flops 4313841664 | bytes 16777216 | tf_op jit(solution)/shard_map/dot_general | solution.py:123
  340.7 11.2 %fusion.10 = bf16[1024,2048]{1,0:T(8,128)(2,1)} fusion(f32[1024,2048]{1,0:T(8,128)S(1)} %copy-done.73, bf16[1024,2048]{0,1:T(8,128)(2,1)S(1)} %copy-done.70, bf16[512,1024]{1,0:T(8,128)(2,1)S(1)} %collective-permute-done.4, bf16[512,1024]{1,0:T(8,128)(2,1)S(1)} %get-tuple-element.197), kind=kOutput, calls=%fused_computation.24 | convolution fusion | flops 4341104640 | bytes 18874368 | tf_op jit(solution)/shard_map/dot_general | solution.py:212
  370.8 10.3 %convolution_convert_fusion.1 = bf16[1024,2048]{1,0:T(8,128)(2,1)} fusion(bf16[512,1024]{1,0:T(8,128)(2,1)S(1)} %copy-done.72, bf16[512,1024]{1,0:T(8,128)(2,1)S(1)} %get-tuple-element.197, f32[1024,2048]{1,0:T(8,128)} %fusion.85), kind=kOutput, calls=%fused_computation.51 | convolution fusion | flops 4320133120 | bytes 14680064 | tf_op jit(solution)/shard_map/dot_general | solution.py:117
  391.4 9.2 %convolution_convert_fusion.2 = bf16[1024,2048]{1,0:T(8,128)(2,1)} fusion(bf16[1024,2048]{1,0:T(8,128)(2,1)} %fusion.10, bf16[512,1024]{1,0:T(8,128)(2,1)} %collective-permute-done, bf16[512,1024]{1,0:T(8,128)(2,1)S(1)} %copy-done.51), kind=kOutput, calls=%fused_computation.52 | convolution fusion | flops 4301258752 | bytes 10485760 | tf_op jit(solution)/shard_map/dot_general | solution.py:117
  400.7 16.4 %all-to-all-done.1 = bf16[4,512,256]{2,1,0:T(8,128)(2,1)S(1)} async-done(((bf16[4,512,256]{2,1,0:T(8,128)(2,1)}), bf16[4,512,256]{2,1,0:T(8,128)(2,1)S(1)}, u32[]{:S(2)}, u32[]{:S(2)}) %all-to-all-start.1) | async-done | bytes 1048608 | tf_op jit(solution)/shard_map/all_to_all | solution.py:224
  431.9 8.2 %multiply_reduce_fusion.2 = (f32[4,512]{1,0:T(4,128)S(1)}, f32[4,512,1024]{2,1,0:T(8,128)}) fusion(f32[4,512,1024]{2,1,0:T(8,128)} %copy-done.1, f32[4,512]{1,0:T(4,128)S(1)} %log_add_fusion.2, bf16[512,4,64]{0,2,1:T(8,128)(2,1)S(1)} %bitcast.237, bf16[1024,4,64]{0,2,1:T(8,128)(2,1)S(1)} %bitcast.246), kind=kOutput, calls=%fused_computation.28 | convolution fusion | flops 274724864 | bytes 17580032 | tf_op jit(solution)/shard_map/qgd,kgd->gqk/dot_general | solution.py:90
  455.3 9.8 %multiply_convert_fusion.1 = bf16[4,512,1536]{2,1,0:T(8,128)(2,1)S(1)} fusion(f32[4,512,1536]{2,1,0:T(8,128)} %get-tuple-element.237, f32[4,512,1536]{2,1,0:T(8,128)} %copy-done, f32[4,512]{1,0:T(4,128)S(1)} %get-tuple-element.236, f32[4,512]{1,0:T(4,128)S(1)} %log_add_fusion.1), kind=kLoop, calls=%fused_computation.8 | loop fusion | flops 12582912 | bytes 31473664 | tf_op jit(solution)/shard_map/convert_element_type | solution.py:94
  471.6 9.1 %multiply_reduce_fusion = (f32[4,512]{1,0:T(4,128)S(1)}, f32[4,512,2048]{2,1,0:T(8,128)}) fusion(f32[4,512,2048]{2,1,0:T(8,128)S(1)} %bitcast.204, f32[4,512]{1,0:T(4,128)S(1)} %log_add_fusion, bf16[512,4,64]{0,2,1:T(8,128)(2,1)} %bitcast.225, bf16[2048,4,64]{0,2,1:T(8,128)(2,1)S(1)} %bitcast.216), kind=kOutput, calls=%fused_computation.1 | convolution fusion | flops 549451776 | bytes 34881536 | tf_op jit(solution)/shard_map/qgd,kgd->gqk/dot_general | solution.py:90
  480.8 10.4 %multiply_convert_fusion = bf16[4,512,2048]{2,1,0:T(8,128)(2,1)} fusion(f32[4,512,2048]{2,1,0:T(8,128)} %get-tuple-element.239, f32[4,512,2048]{2,1,0:T(8,128)S(1)} %bitcast.204, f32[4,512]{1,0:T(4,128)S(1)} %get-tuple-element.238, f32[4,512]{1,0:T(4,128)S(1)} %log_add_fusion), kind=kLoop, calls=%fused_computation | loop fusion | flops 16777216 | bytes 41959424 | tf_op jit(solution)/shard_map/convert_element_type | solution.py:94
  535.7 8.3 %fusion.53 = bf16[2048,4,64]{0,2,1:T(8,128)(2,1)S(1)} fusion(f32[2048,4,64]{0,2,1:T(8,128)} %fusion.47, bf16[512,4,64]{0,2,1:T(8,128)(2,1)S(1)} %bitcast.226, f32[4,512,2048]{2,1,0:T(8,128)} %get-tuple-element.223, f32[4,512]{1,0:T(4,128)S(1)} %log_add_fusion), kind=kOutput, calls=%fused_computation.86 | convolution fusion | flops 546308096 | bytes 20193280 | tf_op jit(solution)/shard_map/gqk,qgd->kgd/dot_general | solution.py:88
  557.3 15.8 %reduce-scatter.23.cloned.1.call-done = bf16[1,256,512]{2,1,0:T(8,128)(2,1)} async-done(((bf16[4,256,512]{2,1,0:T(8,128)(2,1)}), bf16[1,256,512]{2,1,0:T(8,128)(2,1)}) %reduce-scatter.23.cloned.1.call-update) | async-done | bytes 262160 | tf_op jit(solution)/shard_map/reduce_scatter | solution.py:164
  574.2 27.0 %reduce-scatter.19.cloned.1.call-done = bf16[1,256,512]{2,1,0:T(8,128)(2,1)} async-done(((bf16[4,256,512]{2,1,0:T(8,128)(2,1)}), bf16[1,256,512]{2,1,0:T(8,128)(2,1)}) %reduce-scatter.19.cloned.1.call-update) | async-done | bytes 262160 | tf_op jit(solution)/shard_map/reduce_scatter | solution.py:164
  602.9 38.3 %reduce-scatter.11.cloned.1.call-done = bf16[128,768]{1,0:T(8,128)(2,1)} async-done(((bf16[1024,768]{1,0:T(8,128)(2,1)}), bf16[128,768]{1,0:T(8,128)(2,1)}) %reduce-scatter.11.cloned.1.call-update) | async-done | bytes 196624 | tf_op jit(solution)/shard_map/reduce_scatter | solution.py:237
  648.6 71.6 %reduce-scatter.9.cloned.1.call-done = bf16[512,1024]{1,0:T(8,128)(2,1)} async-done(((bf16[2048,1024]{1,0:T(8,128)(2,1)}), bf16[512,1024]{1,0:T(8,128)(2,1)}) %reduce-scatter.9.cloned.1.call-update) | async-done | bytes 1048592 | tf_op jit(solution)/shard_map/reduce_scatter | solution.py:235
  723.9 41.5 %all-reduce.2 = (f32[4,1024]{1,0:T(4,128)}, f32[4,1024]{1,0:T(4,128)}) all-reduce(f32[4,1024]{1,0:T(4,128)S(1)} %pad_maximum_fusion.14, f32[4,1024]{1,0:T(4,128)S(1)} %pad_maximum_fusion.15), channel_id=1, replica_groups=mesh['outer'=4,'pair'=2,'head'=4] {'outer','pair','head'}, use_global_device_ids=true, to_apply=%region_40.41 | all-reduce | flops 8192 | bytes 65536 | tf_op jit(solution)/shard_map/psum | solution.py:240
  (346 shorter events, 230.7 us)
Async XLA Ops:
  7.2 38.8 %all-gather.14.cloned.1.call-start = ((), (), s32[]{:S(2)}) async-start(), calls=%async_computation.13 | async-start | bytes 1310720 | tf_op jit(solution)/shard_map/all_gather | solution.py:156
  8.3 1.5 collective-permute-start.1
  10.7 64.5 %all-gather.18.cloned.1.call-start = ((), (), s32[]{:S(2)}) async-start(), calls=%async_computation.15 | async-start | bytes 1310720 | tf_op jit(solution)/shard_map/all_gather | solution.py:156
  14.0 88.0 %all-gather.10.cloned.1.call-start = ((), (), s32[]{:S(2)}) async-start(), calls=%async_computation.11 | async-start | bytes 1769472 | tf_op jit(solution)/shard_map/all_gather | solution.py:176
  15.7 169.1 %all-gather.8.cloned.1.call-start = ((), (), s32[]{:S(2)}) async-start(), calls=%async_computation.10 | async-start | bytes 5242880 | tf_op jit(solution)/shard_map/all_gather | solution.py:181
  17.9 228.9 %all-gather.12.cloned.1.call-start = ((), (), s32[]{:S(2)}) async-start(), calls=%async_computation.12 | async-start | bytes 2359296 | tf_op jit(solution)/shard_map/all_gather | solution.py:182
  36.7 241.3 %all-gather.16.cloned.1.call-start = ((), (), s32[]{:S(2)}) async-start(), calls=%async_computation.14 | async-start | bytes 5242880 | tf_op jit(solution)/shard_map/all_gather | solution.py:158
  48.4 273.8 %all-gather.20.cloned.1.call-start = ((), (), s32[]{:S(2)}) async-start(), calls=%async_computation.16 | async-start | bytes 5242880 | tf_op jit(solution)/shard_map/all_gather | solution.py:158
  243.3 29.4 %all-to-all-start = ((bf16[4,512,256]{1,2,0:T(8,128)(2,1)}), bf16[4,512,256]{1,2,0:T(8,128)(2,1)S(1)}, u32[]{:S(2)}, u32[]{:S(2)}) async-start(bf16[4,512,256]{1,2,0:T(8,128)(2,1)} %copy.76), calls=%async_computation | async-start | bytes 2097152 | tf_op jit(solution)/shard_map/all_to_all | solution.py:191
  246.8 251.5 %reduce-scatter.13.cloned.1.call-start = ((), (), s32[]{:S(2)}) async-start(), calls=%async_computation.19 | async-start | bytes 2359296 | tf_op jit(solution)/shard_map/reduce_scatter | solution.py:227
  277.9 2.9 collective-permute-start
  331.3 2.7 collective-permute-start.3
  338.1 2.7 collective-permute-start.4
  358.4 2.7 collective-permute-start.5
  370.8 138.0 %reduce-scatter.21.cloned.1.call-start = ((), (), s32[]{:S(2)}) async-start(), calls=%async_computation.23 | async-start | bytes 5242880 | tf_op jit(solution)/shard_map/reduce_scatter | solution.py:162
  386.4 30.6 %all-to-all-start.1 = ((bf16[4,512,256]{2,1,0:T(8,128)(2,1)}), bf16[4,512,256]{2,1,0:T(8,128)(2,1)S(1)}, u32[]{:S(2)}, u32[]{:S(2)}) async-start(bf16[4,512,256]{2,1,0:T(8,128)(2,1)} %bitcast.202), calls=%async_computation.1 | async-start | bytes 2097152 | tf_op jit(solution)/shard_map/all_to_all | solution.py:224
  391.0 142.4 %reduce-scatter.17.cloned.1.call-start = ((), (), s32[]{:S(2)}) async-start(), calls=%async_computation.21 | async-start | bytes 5242880 | tf_op jit(solution)/shard_map/reduce_scatter | solution.py:162
  400.6 155.0 %reduce-scatter.15.cloned.1.call-start = ((), (), s32[]{:S(2)}) async-start(), calls=%async_computation.20 | async-start | bytes 327680 | tf_op jit(solution)/shard_map/reduce_scatter | solution.py:229
  500.1 73.0 %reduce-scatter.23.cloned.1.call-start = ((), (), s32[]{:S(2)}) async-start(), calls=%async_computation.24 | async-start | bytes 1310720 | tf_op jit(solution)/shard_map/reduce_scatter | solution.py:164
  511.3 90.0 %reduce-scatter.19.cloned.1.call-start = ((), (), s32[]{:S(2)}) async-start(), calls=%async_computation.22 | async-start | bytes 1310720 | tf_op jit(solution)/shard_map/reduce_scatter | solution.py:164
  535.6 105.6 %reduce-scatter.11.cloned.1.call-start = ((), (), s32[]{:S(2)}) async-start(), calls=%async_computation.18 | async-start | bytes 1769472 | tf_op jit(solution)/shard_map/reduce_scatter | solution.py:237
  548.8 171.4 %reduce-scatter.9.cloned.1.call-start = ((), (), s32[]{:S(2)}) async-start(), calls=%async_computation.17 | async-start | bytes 5242880 | tf_op jit(solution)/shard_map/reduce_scatter | solution.py:235
  574.1 68.8 %collective-permute-start.7 = (bf16[128,512]{1,0:T(8,128)(2,1)S(1)}, bf16[128,512]{1,0:T(8,128)(2,1)}, u32[]{:S(2)}, u32[]{:S(2)}) collective-permute-start(bf16[128,512]{1,0:T(8,128)(2,1)S(1)} %get-tuple-element.204), channel_id=1, source_target_pairs={{0,4},{4,0},{1,5},{5,1},{2,6},{6,2},{3,7},{7,3},{8,12},{12,8},{9,1... | collective-permute-start | bytes 393224 | tf_op jit(solution)/shard_map/ppermute | solution.py:133
  602.9 43.9 %collective-permute-start.6 = (bf16[128,512]{1,0:T(8,128)(2,1)}, bf16[128,512]{1,0:T(8,128)(2,1)}, u32[]{:S(2)}, u32[]{:S(2)}) collective-permute-start(bf16[128,512]{1,0:T(8,128)(2,1)} %get-tuple-element.206), channel_id=1, source_target_pairs={{0,4},{4,0},{1,5},{5,1},{2,6},{6,2},{3,7},{7,3},{8,12},{12,8},{9,1... | collective-permute-start | bytes 393224 | tf_op jit(solution)/shard_map/ppermute | solution.py:133
  (87 other events, 1522.5 us)
Sparse Core Ops, SparseCore 0:
  10.8 35.2 all-gather.13
  48.2 26.8 all-gather.17
  77.0 24.9 all-gather.9
  104.0 80.7 all-gather.7
  186.5 26.5 all-gather.11
  214.8 52.4 all-gather.15
  269.7 52.4 all-gather.19
  370.9 41.0 reduce-scatter.12
  415.0 52.5 reduce-scatter.20
  470.4 52.5 reduce-scatter.16
  525.3 19.9 reduce-scatter.14
  547.5 25.5 reduce-scatter.22
  575.4 25.7 reduce-scatter.18
  604.4 36.7 reduce-scatter.10
  643.4 76.7 reduce-scatter.8
where the time goes:
time: 779 us; the launch traced here: 776 us
  waiting for transfers between devices  378 us (49%)
  matrix products  190 us (24%)
  other arithmetic  73 us (9%)
  blocking collectives  60.2 us (8%)
  local copies, waits for them, and re-layouts  48.2 us (6%)
  between operations  15.3 us (2%)
  starting transfers between devices  11.2 us (1%)
    all_gather x1, waiting for transfers between devices, on_device(): seq_a = lax.all_gather(norm_a.astype(bf16), 'head', axis=0, tiled=True)  82.8 us
    reduce_scatter x1, waiting for transfers between devices, on_device(): lax.psum_scatter(grad_a, 'head', scatter_dimension=0, tiled=True)  71.6 us
    reduce_scatter x2, waiting for transfers between devices, scatter_half(): block = lax.psum_scatter(blocks, 'head', scatter_dimension=0, tiled=False)  42.9 us
    psum x1, blocking collectives, on_device(): lax.psum((jnp.stack([gain_a, gain_z, gain_c, gain_m]), jnp.stack([bias_a,...  41.5 us
    reduce_scatter x1, waiting for transfers between devices, on_device(): lax.psum_scatter(grad_w, WIDE, scatter_dimension=0, tiled=True)  38.3 us
    all_gather x2, waiting for transfers between devices, gather_half(): columns = lax.all_gather(pair_rows, 'head', axis=0, tiled=False)  31.8 us
    all_gather x2, waiting for transfers between devices, gather_half(): return lax.all_gather(columns, 'outer', axis=0, tiled=True)  31.1 us
    dot_general x4, matrix products, contract_rows(): lax.dot_general(left_op, right_op, (((0,), (0,)), ((), ())), preferred_el...  26.8 us
  transfers between devices with their start and end apart: 25, of which 17 were waited for; matrix products, arithmetic and copies ran while one was open for 32% of the time, Pallas kernels for 0%

commit v1 on v0

--- a/solution.py
+++ b/solution.py
@@ -6,6 +6,19 @@
 
 HD = 64
 EPS = 1e-05
+
+
+def gather_around(x, axis, dim):
+    ways = lax.axis_size(axis)
+    up = [(d, (d + 1) % ways) for d in range(ways)]
+    down = [(d, (d - 1) % ways) for d in range(ways)]
+    earlier, later = ([x], [x])
+    for _ in range(ways // 2):
+        earlier.append(lax.ppermute(earlier[-1], axis, up))
+    for _ in range((ways - 1) // 2):
+        later.append(lax.ppermute(later[-1], axis, down))
+    line = jnp.concatenate([*earlier[::-1], *later[1:]], axis=dim)
+    return jnp.roll(line, (lax.axis_index(axis) - ways // 2) * x.shape[dim], axis=dim)
 
 
 def normalize(values, gain, bias):
@@ -178,7 +191,7 @@
     )
     residual = tokens.astype(jnp.float32)
     norm_a, unit_a, inv_a = normalize(residual, norm_gain[0], norm_bias[0])
-    seq_a = lax.all_gather(norm_a.astype(bf16), "head", axis=0, tiled=True)
+    seq_a = gather_around(norm_a.astype(bf16), "head", 0)
     full_o = lax.all_gather(
         lax.all_gather(w_out, "head", axis=0, tiled=True).T, WIDE, axis=0, tiled=True
     )

time: 779 us -> 725 us (0.931)
  waiting for transfers between devices: 378 us -> 306 us
  starting transfers between devices: 11.2 us -> 21.3 us
  local copies, waits for them, and re-layouts: 48.2 us -> 57.2 us
    all_gather x1 -> x0, waiting for transfers between devices: 82.8 us -> none  [on_device(): seq_a = lax.all_gather(norm_a.astype(bf16), 'head', axis=0, tiled=True)]
    ppermute x0 -> x3, waiting for transfers between devices: none -> 72 us  [the longest x2 72 us: gather_around(): earlier.append(lax.ppermute(earlier[-1], axis, up))]
    all_gather x1, waiting for transfers between devices: 24.6 us -> 0.01 us  [on_device(): lax.all_gather(jnp.concatenate([w_query, w_key, w_value], axis=1), WIDE,...]
    all_gather x2, waiting for transfers between devices: 31.1 us -> 6.91 us  [gather_half(): return lax.all_gather(columns, 'outer', axis=0, tiled=True)]
    all_gather x2, waiting for transfers between devices: 31.8 us -> 9.67 us  [gather_half(): columns = lax.all_gather(pair_rows, 'head', axis=0, tiled=False)]
    ppermute x0 -> x3, starting transfers between devices: none -> 10.3 us  [the longest x2 7.22 us: gather_around(): earlier.append(lax.ppermute(earlier[-1], axis, up))]
    unnamed x175 -> x168, local copies, waits for them, and re-layouts: 18.6 us -> 27.2 us
    reduce_scatter x2, waiting for transfers between devices: 42.9 us -> 50.7 us  [scatter_half(): block = lax.psum_scatter(blocks, 'head', scatter_dimension=0, tiled=False)]
  transfers between devices with their start and end apart: 25 -> 27, of which waited for: 17 -> 17; matrix products, arithmetic and copies ran while one was open for 32% -> 36% of each run, Pallas kernels for 0% -> 0%
where the time goes in v1:
time: 725 us; the launch traced here: 721 us
  waiting for transfers between devices  306 us (42%)
  matrix products  185 us (26%)
  other arithmetic  75.2 us (10%)
  blocking collectives  60.9 us (8%)
  local copies, waits for them, and re-layouts  57.2 us (8%)
  starting transfers between devices  21.3 us (3%)
  between operations  15.2 us (2%)
    ppermute x2, waiting for transfers between devices, gather_around(): earlier.append(lax.ppermute(earlier[-1], axis, up))  72 us
    reduce_scatter x1, waiting for transfers between devices, on_device(): lax.psum_scatter(grad_a, 'head', scatter_dimension=0, tiled=True)  71.6 us
    reduce_scatter x2, waiting for transfers between devices, scatter_half(): block = lax.psum_scatter(blocks, 'head', scatter_dimension=0, tiled=False)  50.7 us
    psum x1, blocking collectives, on_device(): lax.psum((jnp.stack([gain_a, gain_z, gain_c, gain_m]), jnp.stack([bias_a,...  41.5 us
    reduce_scatter x1, waiting for transfers between devices, on_device(): lax.psum_scatter(grad_w, WIDE, scatter_dimension=0, tiled=True)  38.5 us
    dot_general x4, matrix products, contract_rows(): lax.dot_general(left_op, right_op, (((0,), (0,)), ((), ())), preferred_el...  29.1 us
    unnamed x168, local copies, waits for them, and re-layouts  27.2 us
    convert_element_type x4, other arithmetic, attend_back(): grad_scores = (weights * (grad_weights - inner_sum)).astype(jnp.bfloat16)  26.8 us
  transfers between devices with their start and end apart: 27, of which 17 were waited for; matrix products, arithmetic and copies ran while one was open for 36% of the time, Pallas kernels for 0%

profile of v1, /device:TPU:0, one launch (start us, length us, event | category | flops | bytes accessed | tf_op | source)
XLA Modules:
  0.0 720.6 jit_solution(3128145378018568035)
XLA Ops:
  15.8 19.5 %all_gather.24 = bf16[1024,128]{1,0:T(8,128)(2,1)} all-gather(bf16[256,128]{1,0:T(8,128)(2,1)} %param.35), channel_id=1, replica_groups=mesh['outer'=4,'pair'=2,'head'=4] {'head'}, dimensions={0}, use_global_device_ids=true | all-gather | bytes 327680 | tf_op jit(solution)/shard_map/all_gather | solution.py:196
  35.3 9.6 %all-gather.11.cloned.1.call-done = bf16[4,256,512]{2,1,0:T(8,128)(2,1)} async-done(((bf16[1,256,512]{2,1,0:T(8,128)(2,1)}), bf16[4,256,512]{2,1,0:T(8,128)(2,1)}) %all-gather.11.cloned.1.call-update) | async-done | bytes 1048592 | tf_op jit(solution)/shard_map/all_gather | solution.py:169
  55.2 39.2 %collective-permute-done = bf16[512,1024]{1,0:T(8,128)(2,1)} collective-permute-done((bf16[512,1024]{1,0:T(8,128)(2,1)}, bf16[512,1024]{1,0:T(8,128)(2,1)}, u32[]{:S(2)}, u32[]{:S(2)}) %collective-permute-start) | collective-permute-done | bytes 1048608 | tf_op jit(solution)/shard_map/ppermute | solution.py:17
  105.4 32.8 %collective-permute-done.1 = bf16[512,1024]{1,0:T(8,128)(2,1)} collective-permute-done((bf16[512,1024]{1,0:T(8,128)(2,1)}, bf16[512,1024]{1,0:T(8,128)(2,1)}, u32[]{:S(2)}, u32[]{:S(2)}) %collective-permute-start.1) | collective-permute-done | bytes 1048608 | tf_op jit(solution)/shard_map/ppermute | solution.py:17
  185.7 7.8 %fusion.143 = (f32[4,512]{1,0:T(4,128)S(1)}, f32[4,512,2048]{2,1,0:T(8,128)}) fusion(bf16[512,4,64]{0,2,1:T(8,128)(2,1)S(1)} %bitcast.223, bf16[2048,4,64]{0,2,1:T(8,128)(2,1)S(1)} %bitcast.207, pred[512,2048]{1,0:T(8,128)(4,1)S(1)} %iota_compare_fusion), kind=kOutput, calls=%fused_computation.244 | convolution fusion | flops 549451776 | bytes 19144704 | tf_op jit(solution)/shard_map/qgd,kgd->gqk/dot_general | solution.py:44
  193.5 8.2 %fusion = f32[4,512]{1,0:T(4,128)S(1)} fusion(f32[4,512,2048]{2,1,0:T(8,128)} %get-tuple-element.223, f32[4,512]{1,0:T(4,128)S(1)} %get-tuple-element.222), kind=kLoop, calls=%fused_computation.6 | loop fusion | flops 8386560 | bytes 16793600 | tf_op jit(solution)/shard_map/reduce_sum | solution.py:70
  201.8 7.6 %fusion.116 = bf16[512,4,64]{0,2,1:T(8,128)(2,1)S(1)} fusion(bf16[2048,4,64]{0,2,1:T(8,128)(2,1)S(1)} %bitcast.211, f32[4,512,2048]{2,1,0:T(8,128)} %get-tuple-element.223, f32[4,512]{1,0:T(4,128)S(1)} %fusion, f32[4,512]{1,0:T(4,128)S(1)} %get-tuple-element.222), kind=kOutput, calls=%fused_computation.163 | convolution fusion | flops 549584896 | bytes 18104320 | tf_op jit(solution)/shard_map/gqk,kgd->qgd/dot_general | solution.py:73
  216.6 25.1 %all-to-all-done = bf16[4,512,256]{1,2,0:T(8,128)(2,1)S(1)} async-done(((bf16[4,512,256]{1,2,0:T(8,128)(2,1)}), bf16[4,512,256]{1,2,0:T(8,128)(2,1)S(1)}, u32[]{:S(2)}, u32[]{:S(2)}) %all-to-all-start) | async-done | bytes 1048608 | tf_op jit(solution)/shard_map/all_to_all | solution.py:204
  249.8 10.3 %fusion.95 = f32[1024,2048]{1,0:T(8,128)} fusion(bf16[1024,2048]{0,1:T(8,128)(2,1)} %all-gather.13.cloned.1.call-done, bf16[512,1024]{1,0:T(8,128)(2,1)} %collective-permute-done.3, bf16[512,1024]{1,0:T(8,128)(2,1)S(1)} %add_convert_fusion.1), kind=kOutput, calls=%fused_computation.143 | convolution fusion | flops 4299161600 | bytes 14680064 | tf_op jit(solution)/shard_map/dot_general | solution.py:214
  267.1 9.0 %fusion.132 = f32[1024,1024]{1,0:T(8,128)S(1)} fusion(bf16[1024,2048]{0,1:T(8,128)(2,1)} %all-gather.17.cloned.1.call-done, f32[1024,2048]{1,0:T(8,128)} %fusion.95), kind=kOutput, calls=%fused_computation.233 | convolution fusion | flops 4313841664 | bytes 16777216 | tf_op jit(solution)/shard_map/dot_general | solution.py:136
  285.7 11.2 %fusion.10 = bf16[1024,2048]{1,0:T(8,128)(2,1)} fusion(f32[1024,2048]{1,0:T(8,128)S(1)} %copy-done.70, bf16[1024,2048]{0,1:T(8,128)(2,1)S(1)} %copy-done.67, bf16[512,1024]{1,0:T(8,128)(2,1)S(1)} %collective-permute-done.7, bf16[512,1024]{1,0:T(8,128)(2,1)S(1)} %get-tuple-element.197), kind=kOutput, calls=%fused_computation.24 | convolution fusion | flops 4341104640 | bytes 18874368 | tf_op jit(solution)/shard_map/dot_general | solution.py:225
  315.8 10.2 %convolution_convert_fusion.1 = bf16[1024,2048]{1,0:T(8,128)(2,1)} fusion(bf16[512,1024]{1,0:T(8,128)(2,1)S(1)} %copy-done.69, bf16[512,1024]{1,0:T(8,128)(2,1)S(1)} %get-tuple-element.197, f32[1024,2048]{1,0:T(8,128)} %fusion.95), kind=kOutput, calls=%fused_computation.51 | convolution fusion | flops 4320133120 | bytes 14680064 | tf_op jit(solution)/shard_map/dot_general | solution.py:130
  335.3 9.4 %convolution_convert_fusion.2 = bf16[1024,2048]{1,0:T(8,128)(2,1)} fusion(bf16[1024,2048]{1,0:T(8,128)(2,1)} %fusion.10, bf16[512,1024]{1,0:T(8,128)(2,1)} %collective-permute-done.3, bf16[512,1024]{1,0:T(8,128)(2,1)S(1)} %copy-done.49), kind=kOutput, calls=%fused_computation.52 | convolution fusion | flops 4301258752 | bytes 10485760 | tf_op jit(solution)/shard_map/dot_general | solution.py:130
  344.8 16.1 %all-to-all-done.1 = bf16[4,512,256]{2,1,0:T(8,128)(2,1)S(1)} async-done(((bf16[4,512,256]{2,1,0:T(8,128)(2,1)}), bf16[4,512,256]{2,1,0:T(8,128)(2,1)S(1)}, u32[]{:S(2)}, u32[]{:S(2)}) %all-to-all-start.1) | async-done | bytes 1048608 | tf_op jit(solution)/shard_map/all_to_all | solution.py:237
  391.0 10.6 %multiply_convert_fusion.1 = bf16[4,512,1536]{2,1,0:T(8,128)(2,1)S(1)} fusion(f32[4,512,1536]{2,1,0:T(8,128)} %get-tuple-element.237, f32[4,512,1536]{2,1,0:T(8,128)} %copy-done, f32[4,512]{1,0:T(4,128)S(1)} %get-tuple-element.236, f32[4,512]{1,0:T(4,128)S(1)} %log_add_fusion.1), kind=kLoop, calls=%fused_computation.8 | loop fusion | flops 12582912 | bytes 31473664 | tf_op jit(solution)/shard_map/convert_element_type | solution.py:107
  405.8 7.8 %multiply_reduce_fusion = (f32[4,512]{1,0:T(4,128)S(1)}, f32[4,512,2048]{2,1,0:T(8,128)}) fusion(f32[4,512,2048]{2,1,0:T(8,128)S(1)} %bitcast.202, f32[4,512]{1,0:T(4,128)S(1)} %log_add_fusion, bf16[512,4,64]{0,2,1:T(8,128)(2,1)S(1)} %bitcast.221, bf16[2048,4,64]{0,2,1:T(8,128)(2,1)S(1)} %bitcast.212), kind=kOutput, calls=%fused_computation.1 | convolution fusion | flops 549451776 | bytes 34881536 | tf_op jit(solution)/shard_map/qgd,kgd->gqk/dot_general | solution.py:103
  413.6 10.3 %multiply_convert_fusion = bf16[4,512,2048]{2,1,0:T(8,128)(2,1)} fusion(f32[4,512,2048]{2,1,0:T(8,128)} %get-tuple-element.239, f32[4,512,2048]{2,1,0:T(8,128)S(1)} %bitcast.202, f32[4,512]{1,0:T(4,128)S(1)} %get-tuple-element.238, f32[4,512]{1,0:T(4,128)S(1)} %log_add_fusion), kind=kLoop, calls=%fused_computation | loop fusion | flops 16777216 | bytes 41959424 | tf_op jit(solution)/shard_map/convert_element_type | solution.py:107
  457.3 8.5 %fusion.54 = f32[2048,4,64]{0,2,1:T(8,128)} fusion(f32[2048,4,64]{0,2,1:T(8,128)} %fusion.99, bf16[512,4,64]{0,2,1:T(8,128)(2,1)S(1)} %bitcast.230, f32[4,512,1536]{2,1,0:T(8,128)} %copy-done, f32[4,512]{1,0:T(4,128)S(1)} %log_add_fusion.1), kind=kOutput, calls=%fused_computation.88 | convolution fusion | flops 409337856 | bytes 15998976 | tf_op jit(solution)/shard_map/gqk,qgd->kgd/dot_general | solution.py:101
  471.0 8.2 %fusion.60 = bf16[2048,4,64]{0,2,1:T(8,128)(2,1)S(1)} fusion(f32[2048,4,64]{0,2,1:T(8,128)} %fusion.54, bf16[512,4,64]{0,2,1:T(8,128)(2,1)S(1)} %bitcast.222, f32[4,512,2048]{2,1,0:T(8,128)} %get-tuple-element.223, f32[4,512]{1,0:T(4,128)S(1)} %log_add_fusion), kind=kOutput, calls=%fused_computation.90 | convolution fusion | flops 546308096 | bytes 20193280 | tf_op jit(solution)/shard_map/gqk,qgd->kgd/dot_general | solution.py:101
  494.4 23.8 %reduce-scatter.23.cloned.1.call-done = bf16[1,256,512]{2,1,0:T(8,128)(2,1)} async-done(((bf16[4,256,512]{2,1,0:T(8,128)(2,1)}), bf16[1,256,512]{2,1,0:T(8,128)(2,1)}) %reduce-scatter.23.cloned.1.call-update) | async-done | bytes 262160 | tf_op jit(solution)/shard_map/reduce_scatter | solution.py:177
  519.3 26.9 %reduce-scatter.19.cloned.1.call-done = bf16[1,256,512]{2,1,0:T(8,128)(2,1)} async-done(((bf16[4,256,512]{2,1,0:T(8,128)(2,1)}), bf16[1,256,512]{2,1,0:T(8,128)(2,1)}) %reduce-scatter.19.cloned.1.call-update) | async-done | bytes 262160 | tf_op jit(solution)/shard_map/reduce_scatter | solution.py:177
  547.8 38.5 %reduce-scatter.11.cloned.1.call-done = bf16[128,768]{1,0:T(8,128)(2,1)} async-done(((bf16[1024,768]{1,0:T(8,128)(2,1)}), bf16[128,768]{1,0:T(8,128)(2,1)}) %reduce-scatter.11.cloned.1.call-update) | async-done | bytes 196624 | tf_op jit(solution)/shard_map/reduce_scatter | solution.py:250
  593.7 71.6 %reduce-scatter.9.cloned.1.call-done = bf16[512,1024]{1,0:T(8,128)(2,1)} async-done(((bf16[2048,1024]{1,0:T(8,128)(2,1)}), bf16[512,1024]{1,0:T(8,128)(2,1)}) %reduce-scatter.9.cloned.1.call-update) | async-done | bytes 1048592 | tf_op jit(solution)/shard_map/reduce_scatter | solution.py:248
  669.1 41.5 %all-reduce.2 = (f32[4,1024]{1,0:T(4,128)}, f32[4,1024]{1,0:T(4,128)}) all-reduce(f32[4,1024]{1,0:T(4,128)S(1)} %pad_maximum_fusion.14, f32[4,1024]{1,0:T(4,128)S(1)} %pad_maximum_fusion.15), channel_id=1, replica_groups=mesh['outer'=4,'pair'=2,'head'=4] {'outer','pair','head'}, use_global_device_ids=true, to_apply=%region_40.41 | all-reduce | flops 8192 | bytes 65536 | tf_op jit(solution)/shard_map/psum | solution.py:253
  (344 shorter events, 241.7 us)
Async XLA Ops:
  7.2 37.7 %all-gather.11.cloned.1.call-start = ((), (), s32[]{:S(2)}) async-start(), calls=%async_computation.12 | async-start | bytes 1310720 | tf_op jit(solution)/shard_map/all_gather | solution.py:169
  10.7 92.4 %all-gather.15.cloned.1.call-start = ((), (), s32[]{:S(2)}) async-start(), calls=%async_computation.14 | async-start | bytes 1310720 | tf_op jit(solution)/shard_map/all_gather | solution.py:169
  14.0 140.8 %all-gather.7.cloned.1.call-start = ((), (), s32[]{:S(2)}) async-start(), calls=%async_computation.10 | async-start | bytes 1769472 | tf_op jit(solution)/shard_map/all_gather | solution.py:189
  15.7 200.8 %all-gather.9.cloned.1.call-start = ((), (), s32[]{:S(2)}) async-start(), calls=%async_computation.11 | async-start | bytes 2359296 | tf_op jit(solution)/shard_map/all_gather | solution.py:195
  35.2 214.6 %all-gather.13.cloned.1.call-start = ((), (), s32[]{:S(2)}) async-start(), calls=%async_computation.13 | async-start | bytes 5242880 | tf_op jit(solution)/shard_map/all_gather | solution.py:171
  47.2 219.9 %all-gather.17.cloned.1.call-start = ((), (), s32[]{:S(2)}) async-start(), calls=%async_computation.15 | async-start | bytes 5242880 | tf_op jit(solution)/shard_map/all_gather | solution.py:171
  49.4 45.0 %collective-permute-start = (bf16[512,1024]{1,0:T(8,128)(2,1)}, bf16[512,1024]{1,0:T(8,128)(2,1)}, u32[]{:S(2)}, u32[]{:S(2)}) collective-permute-start(bf16[512,1024]{1,0:T(8,128)(2,1)} %fusion.69), channel_id=1, source_target_pairs={{0,1},{1,2},{2,3},{3,0},{4,5},{5,6},{6,7},{7,4},{8,9},{9,10},{10,1... | collective-permute-start | bytes 3145736 | tf_op jit(solution)/shard_map/ppermute | solution.py:17
  50.1 94.0 %collective-permute-start.2 = (bf16[512,1024]{1,0:T(8,128)(2,1)}, bf16[512,1024]{1,0:T(8,128)(2,1)}, u32[]{:S(2)}, u32[]{:S(2)}) collective-permute-start(bf16[512,1024]{1,0:T(8,128)(2,1)} %fusion.69), channel_id=1, source_target_pairs={{0,3},{1,0},{2,1},{3,2},{4,7},{5,4},{6,5},{7,6},{8,11},{9,8},{10,9... | collective-permute-start | bytes 3145736 | tf_op jit(solution)/shard_map/ppermute | solution.py:19
  94.4 43.7 %collective-permute-start.1 = (bf16[512,1024]{1,0:T(8,128)(2,1)}, bf16[512,1024]{1,0:T(8,128)(2,1)}, u32[]{:S(2)}, u32[]{:S(2)}) collective-permute-start(bf16[512,1024]{1,0:T(8,128)(2,1)} %collective-permute-done), channel_id=1, source_target_pairs={{0,1},{1,2},{2,3},{3,0},{4,5},{5,6},{6,7},{7,4},{8,9},{9,10},{10,1... | collective-permute-start | bytes 3145736 | tf_op jit(solution)/shard_map/ppermute | solution.py:17
  213.0 28.7 %all-to-all-start = ((bf16[4,512,256]{1,2,0:T(8,128)(2,1)}), bf16[4,512,256]{1,2,0:T(8,128)(2,1)S(1)}, u32[]{:S(2)}, u32[]{:S(2)}) async-start(bf16[4,512,256]{1,2,0:T(8,128)(2,1)} %copy.76), calls=%async_computation | async-start | bytes 2097152 | tf_op jit(solution)/shard_map/all_to_all | solution.py:204
  216.5 207.4 %reduce-scatter.13.cloned.1.call-start = ((), (), s32[]{:S(2)}) async-start(), calls=%async_computation.18 | async-start | bytes 2359296 | tf_op jit(solution)/shard_map/reduce_scatter | solution.py:240
  247.0 2.9 collective-permute-start.3
  276.2 2.7 collective-permute-start.6
  303.3 2.7 collective-permute-start.8
  315.7 122.7 %reduce-scatter.21.cloned.1.call-start = ((), (), s32[]{:S(2)}) async-start(), calls=%async_computation.22 | async-start | bytes 5242880 | tf_op jit(solution)/shard_map/reduce_scatter | solution.py:175
  330.3 30.7 %all-to-all-start.1 = ((bf16[4,512,256]{2,1,0:T(8,128)(2,1)}), bf16[4,512,256]{2,1,0:T(8,128)(2,1)S(1)}, u32[]{:S(2)}, u32[]{:S(2)}) async-start(bf16[4,512,256]{2,1,0:T(8,128)(2,1)} %bitcast.200), calls=%async_computation.1 | async-start | bytes 2097152 | tf_op jit(solution)/shard_map/all_to_all | solution.py:237
  334.9 133.4 %reduce-scatter.17.cloned.1.call-start = ((), (), s32[]{:S(2)}) async-start(), calls=%async_computation.20 | async-start | bytes 5242880 | tf_op jit(solution)/shard_map/reduce_scatter | solution.py:175
  344.8 148.0 %reduce-scatter.15.cloned.1.call-start = ((), (), s32[]{:S(2)}) async-start(), calls=%async_computation.19 | async-start | bytes 327680 | tf_op jit(solution)/shard_map/reduce_scatter | solution.py:242
  425.8 92.4 %reduce-scatter.23.cloned.1.call-start = ((), (), s32[]{:S(2)}) async-start(), calls=%async_computation.23 | async-start | bytes 1310720 | tf_op jit(solution)/shard_map/reduce_scatter | solution.py:177
  440.9 105.3 %reduce-scatter.19.cloned.1.call-start = ((), (), s32[]{:S(2)}) async-start(), calls=%async_computation.21 | async-start | bytes 1310720 | tf_op jit(solution)/shard_map/reduce_scatter | solution.py:177
  470.5 115.8 %reduce-scatter.11.cloned.1.call-start = ((), (), s32[]{:S(2)}) async-start(), calls=%async_computation.17 | async-start | bytes 1769472 | tf_op jit(solution)/shard_map/reduce_scatter | solution.py:250
  486.2 179.2 %reduce-scatter.9.cloned.1.call-start = ((), (), s32[]{:S(2)}) async-start(), calls=%async_computation.16 | async-start | bytes 5242880 | tf_op jit(solution)/shard_map/reduce_scatter | solution.py:248
  519.2 68.8 %collective-permute-start.10 = (bf16[128,512]{1,0:T(8,128)(2,1)S(1)}, bf16[128,512]{1,0:T(8,128)(2,1)}, u32[]{:S(2)}, u32[]{:S(2)}) collective-permute-start(bf16[128,512]{1,0:T(8,128)(2,1)S(1)} %get-tuple-element.204), channel_id=1, source_target_pairs={{0,4},{4,0},{1,5},{5,1},{2,6},{6,2},{3,7},{7,3},{8,12},{12,8},{9,1... | collective-permute-start | bytes 393224 | tf_op jit(solution)/shard_map/ppermute | solution.py:146
  547.8 44.1 %collective-permute-start.9 = (bf16[128,512]{1,0:T(8,128)(2,1)}, bf16[128,512]{1,0:T(8,128)(2,1)}, u32[]{:S(2)}, u32[]{:S(2)}) collective-permute-start(bf16[128,512]{1,0:T(8,128)(2,1)} %get-tuple-element.206), channel_id=1, source_target_pairs={{0,4},{4,0},{1,5},{5,1},{2,6},{6,2},{3,7},{7,3},{8,12},{12,8},{9,1... | collective-permute-start | bytes 393224 | tf_op jit(solution)/shard_map/ppermute | solution.py:146
  (83 other events, 1806.7 us)
Sparse Core Ops, SparseCore 0:
  10.8 34.1 all-gather.10
  47.1 54.8 all-gather.14
  103.8 24.4 all-gather.6
  130.1 28.0 all-gather.8
  159.9 52.4 all-gather.12
  214.6 52.4 all-gather.16
  315.8 41.0 reduce-scatter.12
  359.9 52.6 reduce-scatter.20
  415.6 52.5 reduce-scatter.16
  470.3 19.9 reduce-scatter.14
  492.6 25.5 reduce-scatter.22
  520.4 25.7 reduce-scatter.18
  549.5 36.8 reduce-scatter.10
  588.5 76.7 reduce-scatter.8
